TPU v7x, 32 devices: a whole 2x2x4 slice. The times are simulated.
32 devices in a mesh: ctx: 8 (over y, x, core), head: 4 (over z).
Axes of the slice: x: 2, y: 2, z: 4, core: 2. Of those that a mesh axis runs over, the one named last changes fastest.
Arguments:
- tokens: bfloat16 [1024, 4096], P('ctx'), may hold values from -8 to 8
- w_query: bfloat16 [4096, 4096], P(None, 'head'), may hold values from -1 to 1
- w_key: bfloat16 [4096, 1024], P(None, 'head'), may hold values from -1 to 1
- w_value: bfloat16 [4096, 1024], P(None, 'head'), may hold values from -0.09375 to 0.09375
- w_out: bfloat16 [4096, 4096], P('head'), may hold values from -0.09375 to 0.09375
- doc_ids: int32 [1024], P('ctx'), may hold values from 0 to 7, never falling along the last dimension, each value on 1 to 640 neighbouring positions
Outputs:
- mixed: bfloat16 [1024, 4096], P('ctx', 'head')
Inputs may be any that keep to these rules, and one draw needn't show every extreme that they name: doc_ids never fall along the context; each document has 1 to 640 tokens and one has exactly 640.
All inputs are finite; a program needn't handle non-finite values.
Results may differ from a plain program's by a relative error of at most 0.011.
Values may be sent and summed in bfloat16 or wider, within the bound.
A program may use at most 128 MiB of HBM per device.

v0:
```python
import math
import jax
import jax.numpy as jnp
from jax import lax
from jax.sharding import PartitionSpec as P

HD = 128


def rotate(vectors, places):
    half_dim = vectors.shape[-1] // 2
    freqs = 500000.0 ** (-2.0 * jnp.arange(half_dim, dtype=jnp.float32) / vectors.shape[-1])
    angles = places.astype(jnp.float32)[:, None] * freqs[None, :]
    cosine = jnp.cos(angles)[:, None, :]
    sine = jnp.sin(angles)[:, None, :]
    first_half = vectors[..., :half_dim]
    second_half = vectors[..., half_dim:]
    return jnp.concatenate(
        [first_half * cosine - second_half * sine, second_half * cosine + first_half * sine],
        axis=-1,
    )


def shards(tokens, w_query, w_key, w_value, w_out, doc_ids):
    tok_rows = tokens.shape[0]
    my_index = lax.axis_index("ctx")
    first_row = my_index * tok_rows
    places = first_row + jnp.arange(tok_rows, dtype=jnp.int32)
    query_heads = w_query.shape[1] // HD
    kv_heads = w_key.shape[1] // HD
    group_size = query_heads // kv_heads
    queries = rotate(
        jnp.dot(tokens, w_query, preferred_element_type=jnp.float32).reshape(
            tok_rows, query_heads, HD
        ),
        places,
    ).astype(jnp.bfloat16)
    queries = queries.reshape(tok_rows, kv_heads, group_size, HD)
    keys_here = rotate(
        jnp.dot(tokens, w_key, preferred_element_type=jnp.float32).reshape(tok_rows, kv_heads, HD),
        places,
    ).astype(jnp.bfloat16)
    values_here = jnp.dot(tokens, w_value, preferred_element_type=jnp.float32).astype(jnp.bfloat16)
    kv_width = kv_heads * HD
    packed = jnp.concatenate([keys_here.reshape(tok_rows, kv_width), values_here], axis=1)
    all_docs = lax.all_gather(doc_ids, "ctx", axis=0, tiled=True)
    query_low = jnp.min(doc_ids)
    query_high = jnp.max(doc_ids)
    query_last = first_row + tok_rows - 1
    score_scale = 1.0 / math.sqrt(HD)
    initial = (
        jnp.full((kv_heads, group_size, tok_rows), -1e30, jnp.float32),
        jnp.zeros((kv_heads, group_size, tok_rows), jnp.float32),
        jnp.zeros((kv_heads, group_size, tok_rows, HD), jnp.float32),
    )
    block_kv = lax.all_gather(packed, "ctx", axis=0, tiled=True)
    key_start = jnp.int32(0)
    key_count = block_kv.shape[0]
    key_start = jnp.asarray(key_start, jnp.int32)
    key_index = jnp.arange(key_count, dtype=jnp.int32)

    def accumulate(inner):
        run_max, run_sum, run_acc = inner
        block_keys = block_kv[:, :kv_width].reshape(key_count, kv_heads, HD)
        block_values = block_kv[:, kv_width:].reshape(key_count, kv_heads, HD)
        allowed = (all_docs[None, :] == doc_ids[:, None]) & (key_index[None, :] <= places[:, None])
        scores = (
            jnp.einsum("tjgd,njd->jgtn", queries, block_keys, preferred_element_type=jnp.float32)
            * score_scale
        )
        scores = jnp.where(allowed, scores, -1e30)
        new_max = jnp.maximum(run_max, jnp.max(scores, axis=-1))
        weights = jnp.exp(scores - new_max[..., None]) * allowed.astype(jnp.float32)
        new_sum = jnp.sum(weights, axis=-1)
        summed = jnp.einsum(
            "jgtn,njd->jgtd",
            weights.astype(jnp.bfloat16),
            block_values,
            preferred_element_type=jnp.float32,
        )
        return (new_max, new_sum, summed)

    touches = (
        (jnp.max(all_docs) >= query_low)
        & (jnp.min(all_docs) <= query_high)
        & (key_start <= query_last)
        & (key_start >= 0)
    )
    state = lax.cond(touches, accumulate, lambda inner: inner, initial)
    run_max, run_sum, run_acc = state
    result = run_acc / run_sum[..., None]
    attended = (
        jnp.transpose(result, (2, 0, 1, 3)).reshape(tok_rows, query_heads * HD).astype(jnp.bfloat16)
    )
    partial_value = jnp.dot(attended, w_out, preferred_element_type=jnp.float32)
    return lax.psum_scatter(
        partial_value.astype(jnp.bfloat16), "head", scatter_dimension=1, tiled=True
    )


def solution(mesh):
    return jax.shard_map(
        shards,
        mesh=mesh,
        in_specs=(
            P("ctx", None),
            P(None, "head"),
            P(None, "head"),
            P(None, "head"),
            P("head", None),
            P("ctx"),
        ),
        out_specs=P("ctx", "head"),
        check_vma=False,
    )
```

profile of v0, /device:TPU:0, one launch (start us, length us, event | category | flops | bytes accessed | tf_op | source)
XLA Modules:
  0.0 87.9 jit_solution(16131842945093330449)
XLA Ops:
  6.5 0.0 copy-start
  6.6 1.6 %copy-done = bf16[4096,256]{1,0:T(8,128)(2,1)S(1)} copy-done((bf16[4096,256]{1,0:T(8,128)(2,1)S(1)}, bf16[4096,256]{1,0:T(8,128)(2,1)}, u32[]{:S(2)}) %copy-start) | copy-done | bytes 2097176
  8.1 1.7 %convolution_convert_fusion.1 = bf16[128,256]{1,0:T(8,128)(2,1)S(1)} fusion(bf16[128,4096]{1,0:T(8,128)(2,1)} %param.8, bf16[4096,256]{1,0:T(8,128)(2,1)S(1)} %copy-done), kind=kOutput, calls=%fused_computation.15 | convolution fusion | flops 268468224 | bytes 3211264 | tf_op jit(solution)/shard_map/dot_general | solution.py:43
  9.8 2.4 %fusion.12 = f32[128,256]{1,0:T(8,128)S(1)} fusion(bf16[128,4096]{1,0:T(8,128)(2,1)} %param.8, bf16[4096,256]{1,0:T(8,128)(2,1)} %param.10), kind=kOutput, calls=%fused_computation.32 | convolution fusion | flops 268435456 | bytes 3276800 | tf_op jit(solution)/shard_map/dot_general | solution.py:40
  12.2 0.1 reshape.135
  12.3 0.3 multiply_cosine_fusion
  12.6 0.3 subtract_convert_fusion.1
  12.9 0.2 pad_maximum_fusion.2
  13.1 0.7 pad_maximum_fusion.1
  13.7 0.0 all-gather.3.cloned.1.call-update
  13.8 0.0 reduce-scatter.2.cloned.1.call-start
  13.8 0.0 copy-done.3
  13.8 10.3 %all-gather = s32[8,1,128]{2,1,0:T(1,128)S(1)} all-gather(s32[1,1,128]{2,1,0:T(1,128)S(1)} %bitcast.55), channel_id=1, replica_groups=mesh['ctx'=8,'head'=4] {'ctx'}, dimensions={0}, use_global_device_ids=true | all-gather | bytes 4608 | tf_op jit(solution)/shard_map/all_gather | solution.py:46
  24.1 0.7 fusion.10
  24.8 0.7 fusion.9
  28.1 4.6 %convolution_bitcast_fusion = f32[16,8,8,128]{3,1,2,0:T(8,128)S(1)} fusion(bf16[128,4096]{1,0:T(8,128)(2,1)S(1)} %copy-done.1, bf16[4096,1024]{1,0:T(8,128)(2,1)} %param.9), kind=kOutput, calls=%fused_computation.14 | convolution fusion | flops 1073741824 | bytes 9961472 | tf_op jit(solution)/shard_map/dot_general | solution.py:33
  32.7 0.1 copy.34
  32.8 0.3 subtract_convert_fusion
  33.2 0.1 pad_maximum_fusion
  33.3 6.7 %all-gather.3.cloned.1.call-done = bf16[1024,512]{1,0:T(8,128)(2,1)} async-done(((bf16[128,512]{1,0:T(8,128)(2,1)}), bf16[1024,512]{1,0:T(8,128)(2,1)}) %all-gather.3.cloned.1.call-update) | async-done | bytes 1048592 | tf_op jit(solution)/shard_map/all_gather | solution.py:56
  40.1 6.8 %conditional.1 = (f32[2,4,128]{2,1,0:T(4,128)S(1)}, f32[2,4,128,128]{2,3,1,0:T(8,128)}) conditional(s32[]{:T(128)} %convert_element_type.43, () %tuple.13, (s32[1024]{0:T(1024)S(1)}, s32[128]{0:T(128)S(1)}, s32[1024]{0:T(1024)S(1)}, s32[]{:T(128)}, s32[128]{0:T(128)S(1)}, /*index=5*/bf16[1024,512]{1,0:T(8,128)(2,1)}, ...), branch_computations={%region_4.0_spmd, %region_5.8_spmd} | conditional | flops 551025792 | bytes 22841392 | solution.py:89
  40.1 1.2 %compare_and_fusion = (pred[128,1024]{0,1:T(8,128)(4,1)S(1)}, f32[128,1024]{0,1:T(8,128)}) fusion(s32[128]{0:T(128)S(1)} %broadcast_add_fusion, s32[128]{0:T(128)S(1)} %get-tuple-element.22, s32[1024]{0:T(1024)S(1)} %get-tuple-element.23, s32[1024]{0:T(1024)S(1)} %get-tuple-element.21), kind=kLoop, calls=%fused_computation.7 | loop fusion | flops 524288 | bytes 664576 | tf_op jit(solution)/shard_map/cond/branch_1_fun/and | solution.py:66
  41.2 1.5 %copy.22 = bf16[1024,512]{0,1:T(8,128)(2,1)S(1)} copy(bf16[1024,512]{1,0:T(8,128)(2,1)} %get-tuple-element.44) | data formatting | bytes 2097152 | tf_op jit(solution)/shard_map
  42.7 0.1 fusion.11
  42.8 0.9 fusion
  43.7 0.1 copy-done.2
  43.8 2.1 %fusion.3 = f32[2,4,128,128]{2,3,1,0:T(8,128)} fusion(bf16[1024,2,128,1]{0,2,3,1:T(8,128)(2,1)S(1)} %bitcast.51, f32[2,1024,128,4]{2,1,3,0:T(8,128)S(1)} %get-tuple-element.56, f32[128,1024]{0,1:T(8,128)S(1)} %copy-done.2, f32[2,4,128]{2,1,0:T(4,128)S(1)} %broadcast_maximum_fusion, pred[128,1024]{0,1:T(8,128)(4,1)S(1)} %get-tuple-element.53), kind=kOutput, calls=%fused_computation.5 | convolution fusion | flops 273678336 | bytes 5902336 | tf_op jit(solution)/shard_map/cond | solution.py:89
  45.8 1.0 %fusion.2 = f32[2,4,128]{2,1,0:T(4,128)S(1)} fusion(f32[2,1024,128,4]{2,1,3,0:T(8,128)S(1)} %get-tuple-element.56, f32[128,1024]{0,1:T(8,128)S(1)} %copy-done.2, f32[2,4,128]{2,1,0:T(4,128)S(1)} %broadcast_maximum_fusion, pred[128,1024]{0,1:T(8,128)(4,1)S(1)} %get-tuple-element.53), kind=kLoop, calls=%fused_computation.4 | loop fusion | flops 5241856 | bytes 4857856 | tf_op jit(solution)/shard_map/cond/branch_1_fun/reduce_sum | solution.py:74
  46.9 1.1 %divide_convert_fusion = bf16[2,4,128,128]{2,3,1,0:T(8,128)(2,1)S(1)} fusion(f32[2,4,128,128]{2,3,1,0:T(8,128)} %get-tuple-element.46, f32[2,4,128]{2,1,0:T(4,128)S(1)} %get-tuple-element.31), kind=kLoop, calls=%fused_computation.16 | loop fusion | flops 262144 | bytes 790528 | tf_op jit(solution)/shard_map/convert_element_type | solution.py:93
  47.9 5.7 %convolution_convert_fusion = bf16[128,4096]{1,0:T(8,128)(2,1)} fusion(bf16[128,1024]{0,1:T(8,128)(2,1)S(1)} %bitcast.48, bf16[1024,4096]{1,0:T(8,128)(2,1)} %param.12), kind=kOutput, calls=%fused_computation.13 | convolution fusion | flops 1074266112 | bytes 9699328 | tf_op jit(solution)/shard_map/dot_general | solution.py:95
  53.6 0.0 reduce-scatter.2.cloned.1.call-update
  53.6 27.4 %reduce-scatter.2.cloned.1.call-done = bf16[128,1024]{1,0:T(8,128)(2,1)} async-done(((bf16[128,4096]{1,0:T(8,128)(2,1)}), bf16[128,1024]{1,0:T(8,128)(2,1)}) %reduce-scatter.2.cloned.1.call-update) | async-done | bytes 262160 | tf_op jit(solution)/shard_map/reduce_scatter | solution.py:96
  (14 shorter events, 0.1 us)
Async XLA Ops:
  6.5 1.6 %copy-start = (bf16[4096,256]{1,0:T(8,128)(2,1)S(1)}, bf16[4096,256]{1,0:T(8,128)(2,1)}, u32[]{:S(2)}) copy-start(bf16[4096,256]{1,0:T(8,128)(2,1)} %param.11) | copy-start | bytes 6291460
  6.5 21.5 %copy-start.1 = (bf16[128,4096]{1,0:T(8,128)(2,1)S(1)}, bf16[128,4096]{1,0:T(8,128)(2,1)}, u32[]{:S(2)}) copy-start(bf16[128,4096]{1,0:T(8,128)(2,1)} %param.8) | copy-start | bytes 3145732
  6.5 7.3 %copy-start.3 = (s32[128]{0:T(128)S(1)}, s32[128]{0:T(128)}, u32[]{:S(2)}) copy-start(s32[128]{0:T(128)} %param.13) | copy-start | bytes 1540
  6.5 33.5 %all-gather.3.cloned.1.call-start = ((), (), s32[]{:S(2)}) async-start(), calls=%async_computation.1 | async-start | bytes 1179648 | tf_op jit(solution)/shard_map/all_gather | solution.py:56
  13.8 67.3 %reduce-scatter.2.cloned.1.call-start = ((), (), s32[]{:S(2)}) async-start(), calls=%async_computation.2 | async-start | bytes 1310720 | tf_op jit(solution)/shard_map/reduce_scatter | solution.py:96
  42.7 1.0 %copy-start.2 = (f32[128,1024]{0,1:T(8,128)S(1)}, f32[128,1024]{0,1:T(8,128)}, u32[]{:S(2)}) copy-start(f32[128,1024]{0,1:T(8,128)} %get-tuple-element.54) | copy-start | bytes 1572868 | tf_op jit(solution)/shard_map/cond
Sparse Core Ops, SparseCore 0:
  13.9 26.1 all-gather.2
  53.8 27.2 reduce-scatter.1
where the time goes:
time: 88.3 us; the launch traced here: 87.9 us
  waiting for transfers between devices  34.2 us (39%)
  matrix products  17.3 us (20%)
  between operations  16.1 us (18%)
  blocking collectives  10.3 us (12%)
  other arithmetic  6.54 us (7%)
  local copies, waits for them, and re-layouts  3.45 us (4%)
    reduce_scatter x1, waiting for transfers between devices, shards(): lax.psum_scatter(partial_value.astype(jnp.bfloat16), 'head', scatter_dime...  27.4 us
    all_gather x1, blocking collectives, shards(): all_docs = lax.all_gather(doc_ids, 'ctx', axis=0, tiled=True)  10.3 us
    all_gather x1, waiting for transfers between devices, shards(): block_kv = lax.all_gather(packed, 'ctx', axis=0, tiled=True)  6.74 us
    dot_general x1, matrix products, shards(): partial_value = jnp.dot(attended, w_out, preferred_element_type=jnp.float32)  5.67 us
    dot_general x1, matrix products, shards(): jnp.dot(tokens, w_query, preferred_element_type=jnp.float32)  4.63 us
    dot_general x1, matrix products, shards(): jnp.dot(tokens, w_key, preferred_element_type=jnp.float32)  2.36 us
    cond x1, matrix products, shards(): state = lax.cond(touches, accumulate, lambda inner: inner, initial)  2.09 us
  transfers between devices with their start and end apart: 2, of which 2 were waited for; matrix products, arithmetic and copies ran while one was open for 8% of the time, Pallas kernels for 0%

commit v1 on v0

--- a/solution.py
+++ b/solution.py
@@ -53,7 +53,12 @@
         jnp.zeros((kv_heads, group_size, tok_rows), jnp.float32),
         jnp.zeros((kv_heads, group_size, tok_rows, HD), jnp.float32),
     )
-    block_kv = lax.all_gather(packed, "ctx", axis=0, tiled=True)
+    ring = [packed]
+    for hop in range(7):
+        ring.append(lax.ppermute(ring[-1], "ctx", [(dev, (dev + 1) % 8) for dev in range(8)]))
+    block_kv = jnp.roll(
+        jnp.concatenate(ring[::-1], axis=0), (lax.axis_index("ctx") + 1) * ring[0].shape[0], axis=0
+    )
     key_start = jnp.int32(0)
     key_count = block_kv.shape[0]
     key_start = jnp.asarray(key_start, jnp.int32)

time: 88.3 us -> 118 us (1.34)
  waiting for transfers between devices: 34.2 us -> 50.5 us
  local copies, waits for them, and re-layouts: 3.45 us -> 18.9 us
  matrix products: 17.3 us -> 14.6 us
    ppermute x0 -> x7, waiting for transfers between devices: none -> 23.4 us  [shards(): lax.ppermute(ring[-1], 'ctx', [(dev, (dev + 1) % 8) for dev in range(8)])]
    unnamed x8 -> x48, local copies, waits for them, and re-layouts: 1.68 us -> 13.1 us
    all_gather x1 -> x0, waiting for transfers between devices: 6.74 us -> none  [shards(): block_kv = lax.all_gather(packed, 'ctx', axis=0, tiled=True)]
    another operation x3, local copies, waits for them, and re-layouts: 1.56 us -> 4.05 us
    dot_general x1, matrix products: 2.36 us -> 0.44 us  [shards(): jnp.dot(tokens, w_key, preferred_element_type=jnp.float32)]
    slice x1, local copies, waits for them, and re-layouts: 0.07 us -> 1.76 us  [accumulate(): block_values = block_kv[:, kv_width:].reshape(key_count, kv_heads, HD)]
  transfers between devices with their start and end apart: 2 -> 8, of which waited for: 2 -> 7; matrix products, arithmetic and copies ran while one was open for 8% -> 6% of each run, Pallas kernels for 0% -> 0%
where the time goes in v1:
time: 118 us; the launch traced here: 117 us
  waiting for transfers between devices  50.5 us (43%)
  local copies, waits for them, and re-layouts  18.9 us (16%)
  between operations  16.3 us (14%)
  matrix products  14.6 us (12%)
  blocking collectives  10.5 us (9%)
  other arithmetic  5.42 us (5%)
    reduce_scatter x1, waiting for transfers between devices, shards(): lax.psum_scatter(partial_value.astype(jnp.bfloat16), 'head', scatter_dime...  27.1 us
    ppermute x7, waiting for transfers between devices, shards(): lax.ppermute(ring[-1], 'ctx', [(dev, (dev + 1) % 8) for dev in range(8)])  23.4 us
    unnamed x48, local copies, waits for them, and re-layouts  13.1 us
    all_gather x1, blocking collectives, shards(): all_docs = lax.all_gather(doc_ids, 'ctx', axis=0, tiled=True)  10.5 us
    dot_general x1, matrix products, shards(): partial_value = jnp.dot(attended, w_out, preferred_element_type=jnp.float32)  5.66 us
    dot_general x1, matrix products, shards(): jnp.dot(tokens, w_query, preferred_element_type=jnp.float32)  4.63 us
    another operation x3, local copies, waits for them, and re-layouts  4.05 us
  transfers between devices with their start and end apart: 8, of which 7 were waited for; matrix products, arithmetic and copies ran while one was open for 6% of the time, Pallas kernels for 0%

profile of v1, /device:TPU:0, one launch (start us, length us, event | category | flops | bytes accessed | tf_op | source)
XLA Modules:
  0.0 117.2 jit_solution(8784656012841685982)
XLA Ops:
  6.6 1.5 %copy-done = bf16[4096,256]{1,0:T(8,128)(2,1)S(1)} copy-done((bf16[4096,256]{1,0:T(8,128)(2,1)S(1)}, bf16[4096,256]{1,0:T(8,128)(2,1)}, u32[]{:S(2)}) %copy-start) | copy-done | bytes 2097176
  8.1 1.7 %convolution_convert_fusion.1 = bf16[128,256]{1,0:T(8,128)(2,1)S(1)} fusion(bf16[128,4096]{1,0:T(8,128)(2,1)} %param.8, bf16[4096,256]{1,0:T(8,128)(2,1)S(1)} %copy-done), kind=kOutput, calls=%fused_computation.16 | convolution fusion | flops 268468224 | bytes 3211264 | tf_op jit(solution)/shard_map/dot_general | solution.py:43
  11.8 5.5 %collective-permute-done = bf16[128,512]{1,0:T(8,128)(2,1)S(1)} collective-permute-done((bf16[128,512]{1,0:T(8,128)(2,1)S(1)}, bf16[128,512]{1,0:T(8,128)(2,1)S(1)}, u32[]{:S(2)}, u32[]{:S(2)}) %collective-permute-start) | collective-permute-done | bytes 131104 | tf_op jit(solution)/shard_map/ppermute | solution.py:58
  17.3 5.3 %collective-permute-done.1 = bf16[128,512]{1,0:T(8,128)(2,1)S(1)} collective-permute-done((bf16[128,512]{1,0:T(8,128)(2,1)S(1)}, bf16[128,512]{1,0:T(8,128)(2,1)S(1)}, u32[]{:S(2)}, u32[]{:S(2)}) %collective-permute-start.1) | collective-permute-done | bytes 131104 | tf_op jit(solution)/shard_map/ppermute | solution.py:58
  22.6 5.3 %collective-permute-done.2 = bf16[128,512]{1,0:T(8,128)(2,1)S(1)} collective-permute-done((bf16[128,512]{1,0:T(8,128)(2,1)S(1)}, bf16[128,512]{1,0:T(8,128)(2,1)S(1)}, u32[]{:S(2)}, u32[]{:S(2)}) %collective-permute-start.2) | collective-permute-done | bytes 131104 | tf_op jit(solution)/shard_map/ppermute | solution.py:58
  27.9 5.3 %collective-permute-done.3 = bf16[128,512]{1,0:T(8,128)(2,1)S(1)} collective-permute-done((bf16[128,512]{1,0:T(8,128)(2,1)S(1)}, bf16[128,512]{1,0:T(8,128)(2,1)S(1)}, u32[]{:S(2)}, u32[]{:S(2)}) %collective-permute-start.3) | collective-permute-done | bytes 131104 | tf_op jit(solution)/shard_map/ppermute | solution.py:58
  33.3 4.6 %convolution_bitcast_fusion = f32[16,8,8,128]{3,1,2,0:T(8,128)S(1)} fusion(bf16[128,4096]{1,0:T(8,128)(2,1)S(1)} %copy-done.1, bf16[4096,1024]{1,0:T(8,128)(2,1)} %param.9), kind=kOutput, calls=%fused_computation.15 | convolution fusion | flops 1073741824 | bytes 9961472 | tf_op jit(solution)/shard_map/dot_general | solution.py:33
  39.2 10.5 %all-gather = s32[8,1,128]{2,1,0:T(1,128)S(1)} all-gather(s32[1,1,128]{2,1,0:T(1,128)S(1)} %bitcast.57), channel_id=1, replica_groups=mesh['ctx'=8,'head'=4] {'ctx'}, dimensions={0}, use_global_device_ids=true | all-gather | bytes 4608 | tf_op jit(solution)/shard_map/all_gather | solution.py:46
  49.7 0.7 fusion.9
  50.8 0.7 fusion.10
  54.4 1.5 %collective-permute-done.6 = bf16[128,512]{1,0:T(8,128)(2,1)} collective-permute-done((bf16[128,512]{1,0:T(8,128)(2,1)S(1)}, bf16[128,512]{1,0:T(8,128)(2,1)}, u32[]{:S(2)}, u32[]{:S(2)}) %collective-permute-start.6) | collective-permute-done | bytes 131104 | tf_op jit(solution)/shard_map/ppermute | solution.py:58
  55.8 1.6 %constant_dynamic-update-slice_fusion.15 = bf16[2048,512]{1,0:T(8,128)(2,1)} fusion(bf16[128,512]{1,0:T(8,128)(2,1)} %collective-permute-done.6), kind=kLoop, calls=%fused_computation.43 | loop fusion | bytes 262144
  57.4 0.7 constant_dynamic-update-slice_fusion.14
  58.1 0.7 constant_dynamic-update-slice_fusion.13
  59.4 0.7 constant_dynamic-update-slice_fusion.11
  60.0 0.7 constant_dynamic-update-slice_fusion.10
  60.7 0.7 constant_dynamic-update-slice_fusion.9
  61.4 0.7 constant_dynamic-update-slice_fusion.8
  62.0 1.6 %constant_dynamic-update-slice_fusion.7 = bf16[2048,512]{1,0:T(8,128)(2,1)} fusion(bf16[2048,512]{1,0:T(8,128)(2,1)} %constant_dynamic-update-slice_fusion.8, bf16[128,512]{1,0:T(8,128)(2,1)} %collective-permute-done.6), kind=kLoop, calls=%fused_computation.35 | loop fusion | bytes 262144
  63.6 0.7 constant_dynamic-update-slice_fusion.6
  64.9 0.7 constant_dynamic-update-slice_fusion.4
  66.2 0.7 constant_dynamic-update-slice_fusion.2
  66.9 0.7 constant_dynamic-update-slice_fusion.1
  67.5 0.7 constant_dynamic-update-slice_fusion
  68.2 9.3 %conditional.1 = (f32[2,4,128]{2,1,0:T(4,128)S(1)}, f32[2,4,128,128]{2,3,1,0:T(8,128)S(1)}) conditional(s32[]{:T(128)} %convert_element_type.49, () %tuple.24, (s32[1024]{0:T(1024)S(1)}, s32[128]{0:T(128)S(1)}, s32[1024]{0:T(1024)S(1)}, s32[]{:T(128)}, s32[128]{0:T(128)S(1)}, /*index=5*/s32[]{:T(128)}, s32[]{:T(128)}, ...), branch_computations={%region_4.5_spmd, %region_5.8_spmd.clone} | conditional | flops 551025792 | bytes 22841540 | solution.py:94
  68.5 4.0 %copy.22 = bf16[2048,512]{0,1:T(8,128)(2,1)} copy(bf16[2048,512]{1,0:T(8,128)(2,1)} %get-tuple-element.183) | data formatting | bytes 4194304 | tf_op jit(solution)/shard_map
  72.5 1.8 %fusion.11 = (bf16[1024,256]{0,1:T(8,128)(2,1)S(1)}, bf16[1024,256]{0,1:T(8,128)(2,1)S(1)}) fusion(bf16[2048,512]{0,1:T(8,128)(2,1)} %copy.22, s32[]{:T(128)S(6)} %select_n.28, s32[]{:T(128)S(6)} %add.59), kind=kLoop, calls=%fused_computation.48 | loop fusion | bytes 2097160 | tf_op jit(solution)/shard_map/cond/branch_1_fun/slice | solution.py:70
  74.3 0.9 fusion
  75.2 1.3 %fusion.3 = f32[2,4,128,128]{2,3,1,0:T(8,128)S(1)} fusion(bf16[1024,2,128,1]{0,2,3,1:T(8,128)(2,1)S(1)} %bitcast.54, f32[2,1024,128,4]{2,1,3,0:T(8,128)S(1)} %get-tuple-element.199, f32[128,1024]{0,1:T(8,128)S(1)} %get-tuple-element.197, f32[2,4,128]{2,1,0:T(4,128)S(1)} %broadcast_maximum_fusion, pred[128,1024]{0,1:T(8,128)(4,1)S(1)} %get-tuple-element.196), kind=kOutput, calls=%fused_computation.5 | convolution fusion | flops 273678336 | bytes 5902336 | tf_op jit(solution)/shard_map/cond | solution.py:94
  76.5 1.0 fusion.2
  77.5 5.7 %convolution_convert_fusion = bf16[128,4096]{1,0:T(8,128)(2,1)} fusion(bf16[128,1024]{0,1:T(8,128)(2,1)S(1)} %bitcast.48, bf16[1024,4096]{1,0:T(8,128)(2,1)} %param.12), kind=kOutput, calls=%fused_computation.14 | convolution fusion | flops 1074266112 | bytes 9699328 | tf_op jit(solution)/shard_map/dot_general | solution.py:100
  83.2 27.1 %reduce-scatter.2.cloned.1.call-done = bf16[128,1024]{1,0:T(8,128)(2,1)} async-done(((bf16[128,4096]{1,0:T(8,128)(2,1)}), bf16[128,1024]{1,0:T(8,128)(2,1)}) %reduce-scatter.2.cloned.1.call-update) | async-done | bytes 262160 | tf_op jit(solution)/shard_map/reduce_scatter | solution.py:101
  (65 shorter events, 6.2 us)
Async XLA Ops:
  6.5 1.6 %copy-start = (bf16[4096,256]{1,0:T(8,128)(2,1)S(1)}, bf16[4096,256]{1,0:T(8,128)(2,1)}, u32[]{:S(2)}) copy-start(bf16[4096,256]{1,0:T(8,128)(2,1)} %param.11) | copy-start | bytes 6291460
  6.5 3.3 %copy-start.1 = (bf16[128,4096]{1,0:T(8,128)(2,1)S(1)}, bf16[128,4096]{1,0:T(8,128)(2,1)}, u32[]{:S(2)}) copy-start(bf16[128,4096]{1,0:T(8,128)(2,1)} %param.8) | copy-start | bytes 3145732
  6.5 103.8 %reduce-scatter.2.cloned.1.call-start = ((), (), s32[]{:S(2)}) async-start(), calls=%async_computation.1 | async-start | bytes 1310720 | tf_op jit(solution)/shard_map/reduce_scatter | solution.py:101
  6.6 3.3 %copy-start.2 = (bf16[4096,256]{1,0:T(8,128)(2,1)S(1)}, bf16[4096,256]{1,0:T(8,128)(2,1)}, u32[]{:S(2)}) copy-start(bf16[4096,256]{1,0:T(8,128)(2,1)} %param.10) | copy-start | bytes 6291460
  9.8 1.4 %copy-start.3 = (bf16[128,256]{1,0:T(8,128)(2,1)}, bf16[128,256]{1,0:T(8,128)(2,1)S(1)}, u32[]{:S(2)}) copy-start(bf16[128,256]{1,0:T(8,128)(2,1)S(1)} %convolution_convert_fusion.1) | copy-start | bytes 196612
  11.2 6.1 %collective-permute-start = (bf16[128,512]{1,0:T(8,128)(2,1)S(1)}, bf16[128,512]{1,0:T(8,128)(2,1)S(1)}, u32[]{:S(2)}, u32[]{:S(2)}) collective-permute-start(bf16[128,512]{1,0:T(8,128)(2,1)S(1)} %pad_maximum_fusion.1), channel_id=1, source_target_pairs={{0,4},{4,8},{8,12},{12,16},{16,20},{20,24},{24,28},{28,0},{1,5},{5... | collective-permute-start | bytes 393224 | tf_op jit(solution)/shard_map/ppermute | solution.py:58
  17.3 15.9 %copy-start.5 = (bf16[128,512]{1,0:T(8,128)(2,1)}, bf16[128,512]{1,0:T(8,128)(2,1)S(1)}, u32[]{:S(2)}) copy-start(bf16[128,512]{1,0:T(8,128)(2,1)S(1)} %collective-permute-done) | copy-start | bytes 393220
  17.3 5.3 %collective-permute-start.1 = (bf16[128,512]{1,0:T(8,128)(2,1)S(1)}, bf16[128,512]{1,0:T(8,128)(2,1)S(1)}, u32[]{:S(2)}, u32[]{:S(2)}) collective-permute-start(bf16[128,512]{1,0:T(8,128)(2,1)S(1)} %collective-permute-done), channel_id=1, source_target_pairs={{0,4},{4,8},{8,12},{12,16},{16,20},{20,24},{24,28},{28,0},{1,5},{5... | collective-permute-start | bytes 393224 | tf_op jit(solution)/shard_map/ppermute | solution.py:58
  22.6 10.6 %copy-start.7 = (bf16[128,512]{1,0:T(8,128)(2,1)}, bf16[128,512]{1,0:T(8,128)(2,1)S(1)}, u32[]{:S(2)}) copy-start(bf16[128,512]{1,0:T(8,128)(2,1)S(1)} %collective-permute-done.1) | copy-start | bytes 393220
  22.6 5.3 %collective-permute-start.2 = (bf16[128,512]{1,0:T(8,128)(2,1)S(1)}, bf16[128,512]{1,0:T(8,128)(2,1)S(1)}, u32[]{:S(2)}, u32[]{:S(2)}) collective-permute-start(bf16[128,512]{1,0:T(8,128)(2,1)S(1)} %collective-permute-done.1), channel_id=1, source_target_pairs={{0,4},{4,8},{8,12},{12,16},{16,20},{20,24},{24,28},{28,0},{1,5},{5... | collective-permute-start | bytes 393224 | tf_op jit(solution)/shard_map/ppermute | solution.py:58
  27.9 5.3 %copy-start.9 = (bf16[128,512]{1,0:T(8,128)(2,1)}, bf16[128,512]{1,0:T(8,128)(2,1)S(1)}, u32[]{:S(2)}) copy-start(bf16[128,512]{1,0:T(8,128)(2,1)S(1)} %collective-permute-done.2) | copy-start | bytes 393220
  27.9 5.3 %collective-permute-start.3 = (bf16[128,512]{1,0:T(8,128)(2,1)S(1)}, bf16[128,512]{1,0:T(8,128)(2,1)S(1)}, u32[]{:S(2)}, u32[]{:S(2)}) collective-permute-start(bf16[128,512]{1,0:T(8,128)(2,1)S(1)} %collective-permute-done.2), channel_id=1, source_target_pairs={{0,4},{4,8},{8,12},{12,16},{16,20},{20,24},{24,28},{28,0},{1,5},{5... | collective-permute-start | bytes 393224 | tf_op jit(solution)/shard_map/ppermute | solution.py:58
  33.2 4.7 %copy-start.11 = (bf16[128,512]{1,0:T(8,128)(2,1)}, bf16[128,512]{1,0:T(8,128)(2,1)S(1)}, u32[]{:S(2)}) copy-start(bf16[128,512]{1,0:T(8,128)(2,1)S(1)} %collective-permute-done.3) | copy-start | bytes 393220
  33.2 5.3 %collective-permute-start.4 = (bf16[128,512]{1,0:T(8,128)(2,1)S(1)}, bf16[128,512]{1,0:T(8,128)(2,1)S(1)}, u32[]{:S(2)}, u32[]{:S(2)}) collective-permute-start(bf16[128,512]{1,0:T(8,128)(2,1)S(1)} %collective-permute-done.3), channel_id=1, source_target_pairs={{0,4},{4,8},{8,12},{12,16},{16,20},{20,24},{24,28},{28,0},{1,5},{5... | collective-permute-start | bytes 393224 | tf_op jit(solution)/shard_map/ppermute | solution.py:58
  37.9 1.3 %copy-start.15 = (s32[128]{0:T(128)S(1)}, s32[128]{0:T(128)}, u32[]{:S(2)}) copy-start(s32[128]{0:T(128)} %param.13) | copy-start | bytes 1540
  38.5 0.7 copy-start.13
  38.5 11.9 %collective-permute-start.5 = (bf16[128,512]{1,0:T(8,128)(2,1)S(1)}, bf16[128,512]{1,0:T(8,128)(2,1)S(1)}, u32[]{:S(2)}, u32[]{:S(2)}) collective-permute-start(bf16[128,512]{1,0:T(8,128)(2,1)S(1)} %collective-permute-done.4), channel_id=1, source_target_pairs={{0,4},{4,8},{8,12},{12,16},{16,20},{20,24},{24,28},{28,0},{1,5},{5... | collective-permute-start | bytes 393224 | tf_op jit(solution)/shard_map/ppermute | solution.py:58
  38.5 20.2 %copy-start.12 = (bf16[128,512]{1,0:T(8,128)(2,1)S(1)}, bf16[128,512]{1,0:T(8,128)(2,1)}, u32[]{:S(2)}) copy-start(bf16[128,512]{1,0:T(8,128)(2,1)} %copy-done.11) | copy-start | bytes 393220
  38.5 20.8 %copy-start.10 = (bf16[128,512]{1,0:T(8,128)(2,1)S(1)}, bf16[128,512]{1,0:T(8,128)(2,1)}, u32[]{:S(2)}) copy-start(bf16[128,512]{1,0:T(8,128)(2,1)} %copy-done.9) | copy-start | bytes 393220
  38.6 21.5 %copy-start.8 = (bf16[128,512]{1,0:T(8,128)(2,1)S(1)}, bf16[128,512]{1,0:T(8,128)(2,1)}, u32[]{:S(2)}) copy-start(bf16[128,512]{1,0:T(8,128)(2,1)} %copy-done.7) | copy-start | bytes 393220
  39.2 21.5 %copy-start.6 = (bf16[128,512]{1,0:T(8,128)(2,1)S(1)}, bf16[128,512]{1,0:T(8,128)(2,1)}, u32[]{:S(2)}) copy-start(bf16[128,512]{1,0:T(8,128)(2,1)} %copy-done.5) | copy-start | bytes 393220
  39.2 22.2 %copy-start.4 = (bf16[128,256]{1,0:T(8,128)(2,1)S(1)}, bf16[128,256]{1,0:T(8,128)(2,1)}, u32[]{:S(2)}) copy-start(bf16[128,256]{1,0:T(8,128)(2,1)} %copy-done.3) | copy-start | bytes 196612
  39.2 18.9 %copy-start.14 = (bf16[128,512]{1,0:T(8,128)(2,1)S(1)}, bf16[128,512]{1,0:T(8,128)(2,1)}, u32[]{:S(2)}) copy-start(bf16[128,512]{1,0:T(8,128)(2,1)} %copy-done.13) | copy-start | bytes 393220
  50.4 5.4 %collective-permute-start.6 = (bf16[128,512]{1,0:T(8,128)(2,1)S(1)}, bf16[128,512]{1,0:T(8,128)(2,1)}, u32[]{:S(2)}, u32[]{:S(2)}) collective-permute-start(bf16[128,512]{1,0:T(8,128)(2,1)S(1)} %collective-permute-done.5), channel_id=1, source_target_pairs={{0,4},{4,8},{8,12},{12,16},{16,20},{20,24},{24,28},{28,0},{1,5},{5... | collective-permute-start | bytes 393224 | tf_op jit(solution)/shard_map/ppermute | solution.py:58
Sparse Core Ops, SparseCore 0:
  83.3 26.9 reduce-scatter.1
